TPU v7x, 32 devices: a whole 2x2x4 slice. The times are simulated.
32 devices in a mesh: grp: 2 (over x), tp: 4 (over y, core), pp: 4 (over z).
Axes of the slice: x: 2, y: 2, z: 4, core: 2. Of those that a mesh axis runs over, the one named last changes fastest.
Arguments:
- tokens: bfloat16 [1024, 8192], P('grp', 'tp'), parts along dimension 0, may hold values from -12 to 12
- gain: bfloat16 [4, 8192], P('pp', 'tp'), may hold values from 0.099609375 to 1.8984375
- q_weight: bfloat16 [4, 8192, 4096], P('pp', None, 'tp'), may hold values from -0.5 to 0.5
- kv_weight: bfloat16 [4, 8192, 2048], P('pp', None, 'tp'), may hold values from -0.5 to 0.5
- out_weight: bfloat16 [4, 4096, 8192], P('pp', None, 'tp'), may hold values from -0.09375 to 0.09375
- page_table: int32 [4, 8, 128], P('pp'), may hold values from 0 to 1023, as said below
- segment_ids: int32 [1024], P('grp'), parts along dimension 0, may hold values from 0 to 2, never falling along the last dimension, each value on 1 to 256 neighbouring positions
Outputs:
- hidden: bfloat16 [1024, 8192], P(('grp', 'pp'), 'tp'), parts along dimension 0
- kv_cache: bfloat16 [4, 2048, 4, 256], P('pp', ('grp', 'tp')), parts along dimension 1
There are 2 independent parts, one for each index of `grp`. A program takes and returns all parts, laid end to end along the dimension named above; an argument that names none is the same for every part. Nothing has to cross between parts.
Inputs may be any that keep to these rules, and one draw needn't show every extreme that they name: `page_table`: every entry of a layer's table is distinct and every one of the 1024 values occurs once. For each layer, head and micro-batch the 16 blocks form a run; in each run half of the devices receive exactly 8 pages and the others none, so each device receives exactly 256 pages of a layer.
All inputs are finite; a program needn't handle non-finite values.
Results may differ from a plain program's by a relative error of at most 0.017.
Values may be sent and summed in bfloat16 or wider, within the bound.
A program may use at most 128 MiB of HBM per device.

v0:
```python
import math
import jax
import jax.numpy as jnp
from jax import lax
from jax.sharding import PartitionSpec as P

MODEL_WIDTH = 8192
HEAD_SIZE = 128
KEY_VALUE_HEADS = 8
MB_TOK = 64
MICRO_BATCHES = 8
PAGE_TOKENS = 4
eps_norm = 1e-05


def partner_2(x, axis, apart):
    return lax.ppermute(x, axis, [(i, i ^ 1 << apart) for i in range(lax.axis_size(axis))])


def shifted(x, axis, by):
    peers = lax.axis_size(axis)
    pairs = [(i, i + by) for i in range(peers) if 0 <= i + by < peers]
    return lax.ppermute(x, axis, pairs)


def from_root(x, axis, root):
    mine = lax.axis_index(axis) == root
    return lax.psum(jnp.where(mine, x, jnp.zeros_like(x)), axis)


def send_pages(kv_own, page_rows, micro_idx, is_live, kv_cache, first_head, tensor_parallel_width):
    row_count = kv_own.shape[0]
    kv_cols = kv_own.shape[1]
    head_width = kv_cache.shape[2]
    cache_page_count = kv_cache.shape[0]
    held_heads = max(1, kv_cols // head_width)
    unit_cols = kv_cols // held_heads
    blocks = row_count // PAGE_TOKENS
    paged_rows = (
        kv_own.reshape(blocks, PAGE_TOKENS, held_heads, unit_cols)
        .transpose(2, 0, 1, 3)
        .reshape(held_heads * blocks, PAGE_TOKENS * unit_cols)
    )
    target_pages = lax.dynamic_slice(
        page_rows, (first_head, micro_idx * blocks), (held_heads, blocks)
    ).reshape(-1)
    device = target_pages // cache_page_count
    cache_page_index = target_pages % cache_page_count
    page_count = held_heads * blocks
    capacity = 2 * page_count // tensor_parallel_width
    onehot = (
        device[:, None] == jnp.arange(tensor_parallel_width, dtype=jnp.int32)[None, :]
    ).astype(jnp.int32)
    earlier = jnp.cumsum(onehot, axis=0) - onehot
    arrival = jnp.sum(earlier * onehot, axis=1)
    position = device * capacity + arrival
    outgoing = (
        jnp.zeros((tensor_parallel_width * capacity, PAGE_TOKENS * unit_cols), jnp.bfloat16)
        .at[position]
        .set(paged_rows)
    )
    labels = (
        jnp.full((tensor_parallel_width * capacity,), cache_page_count, jnp.int32)
        .at[position]
        .set(jnp.where(is_live, cache_page_index, cache_page_count))
    )
    incoming, landing = (
        lax.all_to_all(outgoing, "tp", split_axis=0, concat_axis=0, tiled=True),
        lax.all_to_all(labels, "tp", split_axis=0, concat_axis=0, tiled=True),
    )
    offsets = jnp.arange(tensor_parallel_width, dtype=jnp.int32) * kv_cols % head_width
    lane_ids = jnp.arange(head_width, dtype=jnp.int32)
    within = jnp.arange(unit_cols, dtype=jnp.int32)
    placer = (lane_ids[None, None, :] == offsets[:, None, None] + within[None, :, None]).astype(
        jnp.bfloat16
    )
    spread = jnp.einsum(
        "snw,swv->snv",
        incoming.reshape(tensor_parallel_width, capacity * PAGE_TOKENS, unit_cols),
        placer,
        preferred_element_type=jnp.float32,
    ).astype(jnp.bfloat16)
    return kv_cache.at[landing].add(
        spread.reshape(tensor_parallel_width * capacity, PAGE_TOKENS, head_width), mode="drop"
    )


def body(tokens, gain, q_weight, kv_weight, out_weight, page_table, segment_ids):
    tensor_parallel_width = lax.axis_size("tp")
    pp_size = lax.axis_size("pp")
    tp_rank = lax.axis_index("tp")
    section_idx = lax.axis_index("pp")
    w_query = q_weight[0]
    w_keyval = kv_weight[0]
    w_output = out_weight[0]
    page_rows = page_table[0]
    local_width = tokens.shape[1]
    row_total = tokens.shape[0]
    row_count = MB_TOK
    head_dim = HEAD_SIZE
    kv_cols = w_keyval.shape[1]
    held_heads = max(1, kv_cols // (2 * head_dim))
    q_heads = w_query.shape[1] // head_dim
    per_kv = q_heads // held_heads
    first_head = tp_rank * kv_cols // (2 * head_dim)
    cache_page_count = KEY_VALUE_HEADS * (row_total // PAGE_TOKENS) // tensor_parallel_width
    score_scale = 1.0 / math.sqrt(head_dim)
    step_count = MICRO_BATCHES + pp_size - 1
    key_pos = jnp.arange(row_total, dtype=jnp.int32)

    def add_columns(block_cols):
        return (
            jnp.dot(block_cols, w_query, preferred_element_type=jnp.float32),
            jnp.dot(block_cols, w_keyval, preferred_element_type=jnp.float32),
        )

    def add_outputs(block_cols):
        return jnp.dot(block_cols, w_output, preferred_element_type=jnp.float32)

    def one_step(step_idx, state_tuple):
        received, kv_buffer, kv_cache, collected = state_tuple
        micro_raw = step_idx - section_idx
        is_live = (micro_raw >= 0) & (micro_raw < MICRO_BATCHES)
        micro_idx = jnp.clip(micro_raw, 0, MICRO_BATCHES - 1)
        row_start = micro_idx * row_count
        first_rows = lax.dynamic_slice_in_dim(tokens, row_start, row_count, 0)
        current = jnp.where(section_idx == 0, first_rows, received)
        widened = current.astype(jnp.float32)
        partial_sq = jnp.sum(widened * widened, axis=1, keepdims=True)
        mean_sq = lax.psum(partial_sq, "tp") / MODEL_WIDTH
        normed = (widened * lax.rsqrt(mean_sq + eps_norm) * gain.astype(jnp.float32)).astype(
            jnp.bfloat16
        )
        query_sum, keyval_sum = add_columns(lax.all_gather(normed, "tp", axis=1, tiled=True))
        query_matrix = query_sum.astype(jnp.bfloat16)
        kv_own = keyval_sum.astype(jnp.bfloat16)
        if tensor_parallel_width > KEY_VALUE_HEADS:
            partner = partner_2(kv_own, "tp", 0)
            first_half = tp_rank % 2 == 0
            head_pair = jnp.where(
                first_half,
                jnp.concatenate([kv_own, partner], axis=1),
                jnp.concatenate([partner, kv_own], axis=1),
            )
        else:
            head_pair = kv_own
        kv_cache = send_pages(
            kv_own, page_rows, micro_idx, is_live, kv_cache, first_head, tensor_parallel_width
        )
        refreshed = lax.dynamic_update_slice_in_dim(kv_buffer, head_pair, row_start, 0)
        kv_buffer = jnp.where(is_live, refreshed, kv_buffer)
        kv_view = kv_buffer.reshape(row_total, held_heads, 2, head_dim)
        grouped_queries = query_matrix.reshape(row_count, held_heads, per_kv, head_dim)
        scores = (
            jnp.einsum(
                "qgpd,kgd->gpqk",
                grouped_queries,
                kv_view[:, :, 0],
                preferred_element_type=jnp.float32,
            )
            * score_scale
        )
        query_pos = row_start + jnp.arange(row_count, dtype=jnp.int32)
        seg_query = lax.dynamic_slice_in_dim(segment_ids, row_start, row_count, 0)
        allowed = (key_pos[None, :] <= query_pos[:, None]) & (
            segment_ids[None, :] == seg_query[:, None]
        )
        scores = jnp.where(allowed[None, None], scores, -1e30)
        row_max = jnp.max(scores, axis=-1, keepdims=True)
        raised = jnp.exp(scores - row_max)
        weights = (raised / jnp.sum(raised, axis=-1, keepdims=True)).astype(jnp.bfloat16)
        attended = jnp.einsum(
            "gpqk,kgd->qgpd", weights, kv_view[:, :, 1], preferred_element_type=jnp.float32
        )
        attended = attended.astype(jnp.bfloat16).reshape(row_count, q_heads * head_dim)
        projected = add_outputs(lax.all_gather(attended, "tp", axis=1, tiled=True))
        produced = (widened + projected).astype(jnp.bfloat16)
        placed = lax.dynamic_update_slice_in_dim(collected, produced, row_start, 0)
        collected = jnp.where(is_live & (section_idx == pp_size - 1), placed, collected)
        handed = shifted(produced, "pp", 1)
        return (handed, kv_buffer, kv_cache, collected)

    initial = (
        jnp.zeros((row_count, local_width), jnp.bfloat16),
        jnp.zeros((row_total, held_heads * 2 * head_dim), jnp.bfloat16),
        jnp.zeros((cache_page_count, PAGE_TOKENS, 2 * head_dim), jnp.bfloat16),
        jnp.zeros((row_total, local_width), jnp.bfloat16),
    )
    finished = lax.fori_loop(0, step_count, one_step, initial)
    whole_final = from_root(finished[3], "pp", pp_size - 1)
    share_rows = row_total // pp_size
    hidden = lax.dynamic_slice_in_dim(whole_final, section_idx * share_rows, share_rows, 0)
    return (hidden, finished[2][None])


def solution(mesh):
    placed = (
        P("grp", "tp"),
        P("pp", "tp"),
        P("pp", None, "tp"),
        P("pp", None, "tp"),
        P("pp", None, "tp"),
        P("pp", None, None),
        P("grp"),
    )
    return jax.shard_map(
        body,
        mesh=mesh,
        in_specs=placed,
        out_specs=(P(("grp", "pp"), "tp"), P("pp", ("grp", "tp"), None, None)),
        check_vma=False,
    )
```

profile of v0, /device:TPU:0, one launch (start us, length us, event | category | flops | bytes accessed | tf_op | source)
XLA Modules:
  0.0 928.2 jit_solution(15119671289388943089)
XLA Ops:
  9.8 821.5 %while.22 = (s32[]{:T(128)}, bf16[64,2048]{1,0:T(8,128)(2,1)S(1)}, bf16[512,512]{1,0:T(8,128)(2,1)S(1)}, bf16[256,4,256]{2,1,0:T(4,128)(2,1)S(1)}, bf16[512,2048...) while((s32[]{:T(128)}, bf16[64,2048]{1,0:T(8,128)(2,1)S(1)}, ...), condition=%wide.region_10.11_spmd.clone, body=%wide.region_0.10_spmd.clone.sunk | while | flops 2923866880 | bytes 66799608 | solution.py:189
  11.1 8.4 psum.24
  31.1 6.4 all-gather.2.cloned.1.call-done
  37.5 5.3 dynamic-slice_select_fusion.4
  43.0 8.8 convolution_convert_fusion.6
  54.5 7.2 all_gather.25
  61.6 9.6 %select_dynamic-update-slice_fusion.2 = (bf16[512,2048]{1,0:T(8,128)(2,1)}, bf16[64,2048]{1,0:T(8,128)(2,1)S(1)}) fusion(bf16[512,2048]{1,0:T(8,128)(2,1)} %get-tuple-element.624, s32[]{:T(128)S(6)} %select_n.328, pred[]{:T(512)S(6)} %and.146, bf16[64,4096]{1,0:T(8,128)(2,1)S(1)} %all_gather.25, bf16[4096,2048]{1,0:T(8,128)(2,1)} %get-tuple-element.658, ...), kind=kOutput, calls=%fused_computation.27.clone.1 | convolution fusion | flops 1074266112 | bytes 18350084 | tf_op jit(solution)/shard_map/while/body/eval_jaxpr/dot_general | solution.py:118
  88.7 5.8 psum.24
  106.2 5.6 all-gather.2.cloned.1.call-done
  111.8 5.3 dynamic-slice_select_fusion.4
  117.3 8.8 convolution_convert_fusion.6
  129.2 7.2 all_gather.25
  136.3 9.5 %select_dynamic-update-slice_fusion.2 = (bf16[512,2048]{1,0:T(8,128)(2,1)}, bf16[64,2048]{1,0:T(8,128)(2,1)S(1)}) fusion(bf16[512,2048]{1,0:T(8,128)(2,1)} %get-tuple-element.624, s32[]{:T(128)S(6)} %select_n.328, pred[]{:T(512)S(6)} %and.146, bf16[64,4096]{1,0:T(8,128)(2,1)S(1)} %all_gather.25, bf16[4096,2048]{1,0:T(8,128)(2,1)} %get-tuple-element.658, ...), kind=kOutput, calls=%fused_computation.27.clone.1 | convolution fusion | flops 1074266112 | bytes 18350084 | tf_op jit(solution)/shard_map/while/body/eval_jaxpr/dot_general | solution.py:118
  163.0 5.8 psum.24
  180.5 5.6 all-gather.2.cloned.1.call-done
  186.1 5.3 dynamic-slice_select_fusion.4
  191.6 8.8 convolution_convert_fusion.6
  203.0 7.2 all_gather.25
  210.2 9.5 %select_dynamic-update-slice_fusion.2 = (bf16[512,2048]{1,0:T(8,128)(2,1)}, bf16[64,2048]{1,0:T(8,128)(2,1)S(1)}) fusion(bf16[512,2048]{1,0:T(8,128)(2,1)} %get-tuple-element.624, s32[]{:T(128)S(6)} %select_n.328, pred[]{:T(512)S(6)} %and.146, bf16[64,4096]{1,0:T(8,128)(2,1)S(1)} %all_gather.25, bf16[4096,2048]{1,0:T(8,128)(2,1)} %get-tuple-element.658, ...), kind=kOutput, calls=%fused_computation.27.clone.1 | convolution fusion | flops 1074266112 | bytes 18350084 | tf_op jit(solution)/shard_map/while/body/eval_jaxpr/dot_general | solution.py:118
  237.7 5.8 psum.24
  260.3 5.3 dynamic-slice_select_fusion.4
  265.8 8.8 convolution_convert_fusion.6
  277.6 7.2 all_gather.25
  284.8 9.5 %select_dynamic-update-slice_fusion.2 = (bf16[512,2048]{1,0:T(8,128)(2,1)}, bf16[64,2048]{1,0:T(8,128)(2,1)S(1)}) fusion(bf16[512,2048]{1,0:T(8,128)(2,1)} %get-tuple-element.624, s32[]{:T(128)S(6)} %select_n.328, pred[]{:T(512)S(6)} %and.146, bf16[64,4096]{1,0:T(8,128)(2,1)S(1)} %all_gather.25, bf16[4096,2048]{1,0:T(8,128)(2,1)} %get-tuple-element.658, ...), kind=kOutput, calls=%fused_computation.27.clone.1 | convolution fusion | flops 1074266112 | bytes 18350084 | tf_op jit(solution)/shard_map/while/body/eval_jaxpr/dot_general | solution.py:118
  311.4 5.8 psum.24
  328.9 5.6 all-gather.2.cloned.1.call-done
  334.5 5.3 dynamic-slice_select_fusion.4
  340.0 8.8 convolution_convert_fusion.6
  351.5 7.2 all_gather.25
  358.6 9.5 %select_dynamic-update-slice_fusion.2 = (bf16[512,2048]{1,0:T(8,128)(2,1)}, bf16[64,2048]{1,0:T(8,128)(2,1)S(1)}) fusion(bf16[512,2048]{1,0:T(8,128)(2,1)} %get-tuple-element.624, s32[]{:T(128)S(6)} %select_n.328, pred[]{:T(512)S(6)} %and.146, bf16[64,4096]{1,0:T(8,128)(2,1)S(1)} %all_gather.25, bf16[4096,2048]{1,0:T(8,128)(2,1)} %get-tuple-element.658, ...), kind=kOutput, calls=%fused_computation.27.clone.1 | convolution fusion | flops 1074266112 | bytes 18350084 | tf_op jit(solution)/shard_map/while/body/eval_jaxpr/dot_general | solution.py:118
  386.1 5.8 psum.24
  403.6 5.6 all-gather.2.cloned.1.call-done
  409.2 5.3 dynamic-slice_select_fusion.4
  414.7 8.8 convolution_convert_fusion.6
  426.5 7.2 all_gather.25
  433.7 9.5 %select_dynamic-update-slice_fusion.2 = (bf16[512,2048]{1,0:T(8,128)(2,1)}, bf16[64,2048]{1,0:T(8,128)(2,1)S(1)}) fusion(bf16[512,2048]{1,0:T(8,128)(2,1)} %get-tuple-element.624, s32[]{:T(128)S(6)} %select_n.328, pred[]{:T(512)S(6)} %and.146, bf16[64,4096]{1,0:T(8,128)(2,1)S(1)} %all_gather.25, bf16[4096,2048]{1,0:T(8,128)(2,1)} %get-tuple-element.658, ...), kind=kOutput, calls=%fused_computation.27.clone.1 | convolution fusion | flops 1074266112 | bytes 18350084 | tf_op jit(solution)/shard_map/while/body/eval_jaxpr/dot_general | solution.py:118
  460.4 5.8 psum.24
  477.8 5.6 all-gather.2.cloned.1.call-done
  488.9 8.8 convolution_convert_fusion.6
  500.2 7.2 all_gather.25
  507.4 9.5 %select_dynamic-update-slice_fusion.2 = (bf16[512,2048]{1,0:T(8,128)(2,1)}, bf16[64,2048]{1,0:T(8,128)(2,1)S(1)}) fusion(bf16[512,2048]{1,0:T(8,128)(2,1)} %get-tuple-element.624, s32[]{:T(128)S(6)} %select_n.328, pred[]{:T(512)S(6)} %and.146, bf16[64,4096]{1,0:T(8,128)(2,1)S(1)} %all_gather.25, bf16[4096,2048]{1,0:T(8,128)(2,1)} %get-tuple-element.658, ...), kind=kOutput, calls=%fused_computation.27.clone.1 | convolution fusion | flops 1074266112 | bytes 18350084 | tf_op jit(solution)/shard_map/while/body/eval_jaxpr/dot_general | solution.py:118
  535.0 5.8 psum.24
  552.5 5.5 all-gather.2.cloned.1.call-done
  558.0 5.3 dynamic-slice_select_fusion.4
  563.5 8.8 convolution_convert_fusion.6
  575.3 7.2 all_gather.25
  582.4 9.5 %select_dynamic-update-slice_fusion.2 = (bf16[512,2048]{1,0:T(8,128)(2,1)}, bf16[64,2048]{1,0:T(8,128)(2,1)S(1)}) fusion(bf16[512,2048]{1,0:T(8,128)(2,1)} %get-tuple-element.624, s32[]{:T(128)S(6)} %select_n.328, pred[]{:T(512)S(6)} %and.146, bf16[64,4096]{1,0:T(8,128)(2,1)S(1)} %all_gather.25, bf16[4096,2048]{1,0:T(8,128)(2,1)} %get-tuple-element.658, ...), kind=kOutput, calls=%fused_computation.27.clone.1 | convolution fusion | flops 1074266112 | bytes 18350084 | tf_op jit(solution)/shard_map/while/body/eval_jaxpr/dot_general | solution.py:118
  609.1 5.8 psum.24
  626.5 5.7 all-gather.2.cloned.1.call-done
  632.2 5.3 dynamic-slice_select_fusion.4
  637.7 8.8 convolution_convert_fusion.6
  649.5 7.2 all_gather.25
  656.6 9.5 %select_dynamic-update-slice_fusion.2 = (bf16[512,2048]{1,0:T(8,128)(2,1)}, bf16[64,2048]{1,0:T(8,128)(2,1)S(1)}) fusion(bf16[512,2048]{1,0:T(8,128)(2,1)} %get-tuple-element.624, s32[]{:T(128)S(6)} %select_n.328, pred[]{:T(512)S(6)} %and.146, bf16[64,4096]{1,0:T(8,128)(2,1)S(1)} %all_gather.25, bf16[4096,2048]{1,0:T(8,128)(2,1)} %get-tuple-element.658, ...), kind=kOutput, calls=%fused_computation.27.clone.1 | convolution fusion | flops 1074266112 | bytes 18350084 | tf_op jit(solution)/shard_map/while/body/eval_jaxpr/dot_general | solution.py:118
  683.8 5.8 psum.24
  701.3 5.5 all-gather.2.cloned.1.call-done
  706.8 5.3 dynamic-slice_select_fusion.4
  712.3 8.8 convolution_convert_fusion.6
  724.1 7.2 all_gather.25
  731.2 9.5 %select_dynamic-update-slice_fusion.2 = (bf16[512,2048]{1,0:T(8,128)(2,1)}, bf16[64,2048]{1,0:T(8,128)(2,1)S(1)}) fusion(bf16[512,2048]{1,0:T(8,128)(2,1)} %get-tuple-element.624, s32[]{:T(128)S(6)} %select_n.328, pred[]{:T(512)S(6)} %and.146, bf16[64,4096]{1,0:T(8,128)(2,1)S(1)} %all_gather.25, bf16[4096,2048]{1,0:T(8,128)(2,1)} %get-tuple-element.658, ...), kind=kOutput, calls=%fused_computation.27.clone.1 | convolution fusion | flops 1074266112 | bytes 18350084 | tf_op jit(solution)/shard_map/while/body/eval_jaxpr/dot_general | solution.py:118
  758.4 5.8 psum.24
  786.4 8.8 convolution_convert_fusion.6
  798.2 7.2 all_gather.25
  805.4 9.5 %select_dynamic-update-slice_fusion.2 = (bf16[512,2048]{1,0:T(8,128)(2,1)}, bf16[64,2048]{1,0:T(8,128)(2,1)S(1)}) fusion(bf16[512,2048]{1,0:T(8,128)(2,1)} %get-tuple-element.624, s32[]{:T(128)S(6)} %select_n.328, pred[]{:T(512)S(6)} %and.146, bf16[64,4096]{1,0:T(8,128)(2,1)S(1)} %all_gather.25, bf16[4096,2048]{1,0:T(8,128)(2,1)} %get-tuple-element.658, ...), kind=kOutput, calls=%fused_computation.27.clone.1 | convolution fusion | flops 1074266112 | bytes 18350084 | tf_op jit(solution)/shard_map/while/body/eval_jaxpr/dot_general | solution.py:118
  832.9 86.3 %all-reduce.2.cloned.1.call-done = bf16[512,2048]{1,0:T(8,128)(2,1)} async-done(((bf16[512,2048]{1,0:T(8,128)(2,1)}), bf16[512,2048]{1,0:T(8,128)(2,1)}) %all-reduce.2.cloned.1.call-update) | async-done | bytes 2097168 | tf_op jit(solution)/shard_map/psum | solution.py:28
  (579 shorter events, 378.1 us)
Async XLA Ops:
  8.0 1.8 copy-start.2
  8.0 1.8 copy-start.3
  9.8 27.7 %all-gather.2.cloned.1.call-start = ((), (), s32[]{:S(2)}) async-start(), calls=%async_computation.3 | async-start | bytes 1310720 | tf_op jit(solution)/shard_map/while/body/eval_jaxpr/all_gather | solution.py:134
  23.0 6.9 all-to-all-start
  37.5 5.5 copy-start
  71.2 16.3 %collective-permute-start = (bf16[64,2048]{1,0:T(8,128)(2,1)S(1)}, bf16[64,2048]{1,0:T(8,128)(2,1)S(1)}, u32[]{:S(2)}, u32[]{:S(2)}) collective-permute-start(bf16[64,2048]{1,0:T(8,128)(2,1)S(1)} %get-tuple-element.589), channel_id=1, source_target_pairs={{0,1},{1,2},{2,3},{4,5},{5,6},{6,7},{8,9},{9,10},{10,11},{12,13},{... | collective-permute-start | bytes 786440 | tf_op jit(solution)/shard_map/while/body/eval_jaxpr/ppermute | solution.py:23
  76.0 7.9 all-to-all-start.1
  87.5 24.3 %all-gather.2.cloned.1.call-start = ((), (), s32[]{:S(2)}) async-start(), calls=%async_computation.3 | async-start | bytes 1310720 | tf_op jit(solution)/shard_map/while/body/eval_jaxpr/all_gather | solution.py:134
  98.0 6.9 all-to-all-start
  111.8 5.5 copy-start
  145.9 15.9 %collective-permute-start = (bf16[64,2048]{1,0:T(8,128)(2,1)S(1)}, bf16[64,2048]{1,0:T(8,128)(2,1)S(1)}, u32[]{:S(2)}, u32[]{:S(2)}) collective-permute-start(bf16[64,2048]{1,0:T(8,128)(2,1)S(1)} %get-tuple-element.589), channel_id=1, source_target_pairs={{0,1},{1,2},{2,3},{4,5},{5,6},{6,7},{8,9},{9,10},{10,11},{12,13},{... | collective-permute-start | bytes 786440 | tf_op jit(solution)/shard_map/while/body/eval_jaxpr/ppermute | solution.py:23
  150.3 7.9 all-to-all-start.1
  161.8 24.3 %all-gather.2.cloned.1.call-start = ((), (), s32[]{:S(2)}) async-start(), calls=%async_computation.3 | async-start | bytes 1310720 | tf_op jit(solution)/shard_map/while/body/eval_jaxpr/all_gather | solution.py:134
  172.3 6.9 all-to-all-start
  186.1 5.5 copy-start
  219.7 16.7 %collective-permute-start = (bf16[64,2048]{1,0:T(8,128)(2,1)S(1)}, bf16[64,2048]{1,0:T(8,128)(2,1)S(1)}, u32[]{:S(2)}, u32[]{:S(2)}) collective-permute-start(bf16[64,2048]{1,0:T(8,128)(2,1)S(1)} %get-tuple-element.589), channel_id=1, source_target_pairs={{0,1},{1,2},{2,3},{4,5},{5,6},{6,7},{8,9},{9,10},{10,11},{12,13},{... | collective-permute-start | bytes 786440 | tf_op jit(solution)/shard_map/while/body/eval_jaxpr/ppermute | solution.py:23
  225.0 7.9 all-to-all-start.1
  236.5 23.8 %all-gather.2.cloned.1.call-start = ((), (), s32[]{:S(2)}) async-start(), calls=%async_computation.3 | async-start | bytes 1310720 | tf_op jit(solution)/shard_map/while/body/eval_jaxpr/all_gather | solution.py:134
  247.0 6.9 all-to-all-start
  260.3 5.5 copy-start
  294.3 15.9 %collective-permute-start = (bf16[64,2048]{1,0:T(8,128)(2,1)S(1)}, bf16[64,2048]{1,0:T(8,128)(2,1)S(1)}, u32[]{:S(2)}, u32[]{:S(2)}) collective-permute-start(bf16[64,2048]{1,0:T(8,128)(2,1)S(1)} %get-tuple-element.589), channel_id=1, source_target_pairs={{0,1},{1,2},{2,3},{4,5},{5,6},{6,7},{8,9},{9,10},{10,11},{12,13},{... | collective-permute-start | bytes 786440 | tf_op jit(solution)/shard_map/while/body/eval_jaxpr/ppermute | solution.py:23
  298.8 7.9 all-to-all-start.1
  310.2 24.3 %all-gather.2.cloned.1.call-start = ((), (), s32[]{:S(2)}) async-start(), calls=%async_computation.3 | async-start | bytes 1310720 | tf_op jit(solution)/shard_map/while/body/eval_jaxpr/all_gather | solution.py:134
  320.7 6.9 all-to-all-start
  334.5 5.5 copy-start
  368.2 16.7 %collective-permute-start = (bf16[64,2048]{1,0:T(8,128)(2,1)S(1)}, bf16[64,2048]{1,0:T(8,128)(2,1)S(1)}, u32[]{:S(2)}, u32[]{:S(2)}) collective-permute-start(bf16[64,2048]{1,0:T(8,128)(2,1)S(1)} %get-tuple-element.589), channel_id=1, source_target_pairs={{0,1},{1,2},{2,3},{4,5},{5,6},{6,7},{8,9},{9,10},{10,11},{12,13},{... | collective-permute-start | bytes 786440 | tf_op jit(solution)/shard_map/while/body/eval_jaxpr/ppermute | solution.py:23
  373.4 7.9 all-to-all-start.1
  384.9 24.3 %all-gather.2.cloned.1.call-start = ((), (), s32[]{:S(2)}) async-start(), calls=%async_computation.3 | async-start | bytes 1310720 | tf_op jit(solution)/shard_map/while/body/eval_jaxpr/all_gather | solution.py:134
  395.4 6.9 all-to-all-start
  409.2 5.5 copy-start
  443.2 15.9 %collective-permute-start = (bf16[64,2048]{1,0:T(8,128)(2,1)S(1)}, bf16[64,2048]{1,0:T(8,128)(2,1)S(1)}, u32[]{:S(2)}, u32[]{:S(2)}) collective-permute-start(bf16[64,2048]{1,0:T(8,128)(2,1)S(1)} %get-tuple-element.589), channel_id=1, source_target_pairs={{0,1},{1,2},{2,3},{4,5},{5,6},{6,7},{8,9},{9,10},{10,11},{12,13},{... | collective-permute-start | bytes 786440 | tf_op jit(solution)/shard_map/while/body/eval_jaxpr/ppermute | solution.py:23
  447.7 7.9 all-to-all-start.1
  459.1 24.2 %all-gather.2.cloned.1.call-start = ((), (), s32[]{:S(2)}) async-start(), calls=%async_computation.3 | async-start | bytes 1310720 | tf_op jit(solution)/shard_map/while/body/eval_jaxpr/all_gather | solution.py:134
  469.6 6.9 all-to-all-start
  483.4 5.5 copy-start
  516.9 16.8 %collective-permute-start = (bf16[64,2048]{1,0:T(8,128)(2,1)S(1)}, bf16[64,2048]{1,0:T(8,128)(2,1)S(1)}, u32[]{:S(2)}, u32[]{:S(2)}) collective-permute-start(bf16[64,2048]{1,0:T(8,128)(2,1)S(1)} %get-tuple-element.589), channel_id=1, source_target_pairs={{0,1},{1,2},{2,3},{4,5},{5,6},{6,7},{8,9},{9,10},{10,11},{12,13},{... | collective-permute-start | bytes 786440 | tf_op jit(solution)/shard_map/while/body/eval_jaxpr/ppermute | solution.py:23
  522.3 7.9 all-to-all-start.1
  533.7 24.2 %all-gather.2.cloned.1.call-start = ((), (), s32[]{:S(2)}) async-start(), calls=%async_computation.3 | async-start | bytes 1310720 | tf_op jit(solution)/shard_map/while/body/eval_jaxpr/all_gather | solution.py:134
  544.3 6.9 all-to-all-start
  558.0 5.5 copy-start
  592.0 15.9 %collective-permute-start = (bf16[64,2048]{1,0:T(8,128)(2,1)S(1)}, bf16[64,2048]{1,0:T(8,128)(2,1)S(1)}, u32[]{:S(2)}, u32[]{:S(2)}) collective-permute-start(bf16[64,2048]{1,0:T(8,128)(2,1)S(1)} %get-tuple-element.589), channel_id=1, source_target_pairs={{0,1},{1,2},{2,3},{4,5},{5,6},{6,7},{8,9},{9,10},{10,11},{12,13},{... | collective-permute-start | bytes 786440 | tf_op jit(solution)/shard_map/while/body/eval_jaxpr/ppermute | solution.py:23
  596.4 7.9 all-to-all-start.1
  607.9 24.3 %all-gather.2.cloned.1.call-start = ((), (), s32[]{:S(2)}) async-start(), calls=%async_computation.3 | async-start | bytes 1310720 | tf_op jit(solution)/shard_map/while/body/eval_jaxpr/all_gather | solution.py:134
  618.4 6.9 all-to-all-start
  632.2 5.5 copy-start
  666.2 16.4 %collective-permute-start = (bf16[64,2048]{1,0:T(8,128)(2,1)S(1)}, bf16[64,2048]{1,0:T(8,128)(2,1)S(1)}, u32[]{:S(2)}, u32[]{:S(2)}) collective-permute-start(bf16[64,2048]{1,0:T(8,128)(2,1)S(1)} %get-tuple-element.589), channel_id=1, source_target_pairs={{0,1},{1,2},{2,3},{4,5},{5,6},{6,7},{8,9},{9,10},{10,11},{12,13},{... | collective-permute-start | bytes 786440 | tf_op jit(solution)/shard_map/while/body/eval_jaxpr/ppermute | solution.py:23
  671.0 7.9 all-to-all-start.1
  682.6 24.2 %all-gather.2.cloned.1.call-start = ((), (), s32[]{:S(2)}) async-start(), calls=%async_computation.3 | async-start | bytes 1310720 | tf_op jit(solution)/shard_map/while/body/eval_jaxpr/all_gather | solution.py:134
  693.1 6.9 all-to-all-start
  706.8 5.5 copy-start
  740.8 16.4 %collective-permute-start = (bf16[64,2048]{1,0:T(8,128)(2,1)S(1)}, bf16[64,2048]{1,0:T(8,128)(2,1)S(1)}, u32[]{:S(2)}, u32[]{:S(2)}) collective-permute-start(bf16[64,2048]{1,0:T(8,128)(2,1)S(1)} %get-tuple-element.589), channel_id=1, source_target_pairs={{0,1},{1,2},{2,3},{4,5},{5,6},{6,7},{8,9},{9,10},{10,11},{12,13},{... | collective-permute-start | bytes 786440 | tf_op jit(solution)/shard_map/while/body/eval_jaxpr/ppermute | solution.py:23
  745.6 7.9 all-to-all-start.1
  757.2 23.8 %all-gather.2.cloned.1.call-start = ((), (), s32[]{:S(2)}) async-start(), calls=%async_computation.3 | async-start | bytes 1310720 | tf_op jit(solution)/shard_map/while/body/eval_jaxpr/all_gather | solution.py:134
  767.7 6.9 all-to-all-start
  780.9 5.5 copy-start
  814.9 16.4 %collective-permute-start = (bf16[64,2048]{1,0:T(8,128)(2,1)S(1)}, bf16[64,2048]{1,0:T(8,128)(2,1)S(1)}, u32[]{:S(2)}, u32[]{:S(2)}) collective-permute-start(bf16[64,2048]{1,0:T(8,128)(2,1)S(1)} %get-tuple-element.589), channel_id=1, source_target_pairs={{0,1},{1,2},{2,3},{4,5},{5,6},{6,7},{8,9},{9,10},{10,11},{12,13},{... | collective-permute-start | bytes 786440 | tf_op jit(solution)/shard_map/while/body/eval_jaxpr/ppermute | solution.py:23
  819.8 7.9 all-to-all-start.1
  831.3 1.6 copy-start.1
  831.3 87.9 %all-reduce.2.cloned.1.call-start = ((), (), s32[]{:S(2)}) async-start(), calls=%async_computation.2 | async-start | bytes 4194304 | tf_op jit(solution)/shard_map/psum | solution.py:28
Sparse Core Ops, SparseCore 0:
  20.5 17.0 all-gather.1
  95.5 16.2 all-gather.1
  169.8 16.2 all-gather.1
  244.5 15.7 all-gather.1
  318.2 16.2 all-gather.1
  392.9 16.2 all-gather.1
  467.1 16.2 all-gather.1
  541.8 16.1 all-gather.1
  615.9 16.3 all-gather.1
  690.6 16.1 all-gather.1
  765.1 15.7 all-gather.1
Sparse Core Ops, SparseCore 1:
  834.2 85.0 all-reduce.1
where the time goes:
time: 932 us; the launch traced here: 928 us
  matrix products  285 us (31%)
  waiting for transfers between devices  231 us (25%)
  blocking collectives  145 us (16%)
  starting transfers between devices  110 us (12%)
  other arithmetic  70.3 us (8%)
  local copies, waits for them, and re-layouts  69.7 us (7%)
  between operations  15.2 us (2%)
    dot_general x11, matrix products, add_outputs(): return jnp.dot(block_cols, w_output, preferred_element_type=jnp.float32)  105 us
    dot_general x11, matrix products, add_columns(): jnp.dot(block_cols, w_query, preferred_element_type=jnp.float32)  96.7 us
    psum x1, waiting for transfers between devices, from_root(): return lax.psum(jnp.where(mine, x, jnp.zeros_like(x)), axis)  86.3 us
    all_gather x11, blocking collectives, one_step(): projected = add_outputs(lax.all_gather(attended, 'tp', axis=1, tiled=True))  78.7 us
    psum x11, blocking collectives, one_step(): mean_sq = lax.psum(partial_sq, 'tp') / MODEL_WIDTH  66.2 us
    all_gather x11, waiting for transfers between devices, one_step(): lax.all_gather(normed, 'tp', axis=1, tiled=True)  61.4 us
    dot_general x11, matrix products, add_columns(): jnp.dot(block_cols, w_keyval, preferred_element_type=jnp.float32)  58.8 us
    all_to_all x11, waiting for transfers between devices, send_pages(): lax.all_to_all(outgoing, 'tp', split_axis=0, concat_axis=0, tiled=True)  47.7 us
  transfers between devices with their start and end apart: 45, of which 34 were waited for; matrix products, arithmetic and copies ran while one was open for 10% of the time, Pallas kernels for 0%

commit v1 on v0

--- a/solution.py
+++ b/solution.py
@@ -127,7 +127,7 @@
         current = jnp.where(section_idx == 0, first_rows, received)
         widened = current.astype(jnp.float32)
         partial_sq = jnp.sum(widened * widened, axis=1, keepdims=True)
-        mean_sq = lax.psum(partial_sq, "tp") / MODEL_WIDTH
+        mean_sq = jnp.sum(lax.all_gather(partial_sq, "tp"), axis=0) / MODEL_WIDTH
         normed = (widened * lax.rsqrt(mean_sq + eps_norm) * gain.astype(jnp.float32)).astype(
             jnp.bfloat16
         )

time: 932 us -> 949 us (1.018)
  local copies, waits for them, and re-layouts: 69.7 us -> 79.7 us
    psum x11 -> x0, blocking collectives: 66.2 us -> none  [one_step(): mean_sq = lax.psum(partial_sq, 'tp') / MODEL_WIDTH]
    while x0 -> x11, blocking collectives: none -> 65.8 us
where the time goes in v1:
time: 949 us; the launch traced here: 946 us
  matrix products  285 us (30%)
  waiting for transfers between devices  231 us (24%)
  blocking collectives  144 us (15%)
  starting transfers between devices  110 us (12%)
  local copies, waits for them, and re-layouts  79.7 us (8%)
  other arithmetic  70.6 us (7%)
  between operations  15.3 us (2%)
  loops' own time  10.2 us (1%)
    dot_general x11, matrix products, add_outputs(): return jnp.dot(block_cols, w_output, preferred_element_type=jnp.float32)  105 us
    dot_general x11, matrix products, add_columns(): jnp.dot(block_cols, w_query, preferred_element_type=jnp.float32)  96.7 us
    psum x1, waiting for transfers between devices, from_root(): return lax.psum(jnp.where(mine, x, jnp.zeros_like(x)), axis)  86.3 us
    all_gather x11, blocking collectives, one_step(): projected = add_outputs(lax.all_gather(attended, 'tp', axis=1, tiled=True))  78.7 us
    while x11, blocking collectives  65.8 us
    all_gather x11, waiting for transfers between devices, one_step(): lax.all_gather(normed, 'tp', axis=1, tiled=True)  61.4 us
    dot_general x11, matrix products, add_columns(): jnp.dot(block_cols, w_keyval, preferred_element_type=jnp.float32)  58.8 us
    all_to_all x11, waiting for transfers between devices, send_pages(): lax.all_to_all(outgoing, 'tp', split_axis=0, concat_axis=0, tiled=True)  47.7 us
  transfers between devices with their start and end apart: 45, of which 34 were waited for; matrix products, arithmetic and copies ran while one was open for 10% of the time, Pallas kernels for 0%

profile of v1, /device:TPU:0, one launch (start us, length us, event | category | flops | bytes accessed | tf_op | source)
XLA Modules:
  0.0 945.5 jit_solution(11369186242155032917)
XLA Ops:
  9.8 838.7 %while.22 = (s32[]{:T(128)}, bf16[64,2048]{1,0:T(8,128)(2,1)S(1)}, bf16[512,512]{1,0:T(8,128)(2,1)S(1)}, bf16[256,4,256]{2,1,0:T(4,128)(2,1)S(1)}, bf16[512,2048...) while((s32[]{:T(128)}, bf16[64,2048]{1,0:T(8,128)(2,1)S(1)}, ...), condition=%wide.region_10.11_spmd.clone, body=%wide.region_0.10_spmd.clone.sunk | while | flops 2923866880 | bytes 66806104 | solution.py:189
  12.6 8.4 all-reduce.3
  32.7 6.4 all-gather.3.cloned.1.call-done
  39.1 5.3 dynamic-slice_select_fusion.4
  44.6 8.8 convolution_convert_fusion.6
  56.0 7.2 all_gather.35
  63.2 9.6 %select_dynamic-update-slice_fusion.2 = (bf16[512,2048]{1,0:T(8,128)(2,1)}, bf16[64,2048]{1,0:T(8,128)(2,1)S(1)}) fusion(bf16[512,2048]{1,0:T(8,128)(2,1)} %get-tuple-element.644, s32[]{:T(128)S(6)} %select_n.328, pred[]{:T(512)S(6)} %and.146, bf16[64,4096]{1,0:T(8,128)(2,1)S(1)} %all_gather.35, bf16[4096,2048]{1,0:T(8,128)(2,1)} %get-tuple-element.682, ...), kind=kOutput, calls=%fused_computation.27.clone.1 | convolution fusion | flops 1074266112 | bytes 18350084 | tf_op jit(solution)/shard_map/while/body/eval_jaxpr/dot_general | solution.py:118
  91.8 5.8 all-reduce.3
  109.3 5.6 all-gather.3.cloned.1.call-done
  120.4 8.8 convolution_convert_fusion.6
  132.3 7.2 all_gather.35
  139.5 9.5 %select_dynamic-update-slice_fusion.2 = (bf16[512,2048]{1,0:T(8,128)(2,1)}, bf16[64,2048]{1,0:T(8,128)(2,1)S(1)}) fusion(bf16[512,2048]{1,0:T(8,128)(2,1)} %get-tuple-element.644, s32[]{:T(128)S(6)} %select_n.328, pred[]{:T(512)S(6)} %and.146, bf16[64,4096]{1,0:T(8,128)(2,1)S(1)} %all_gather.35, bf16[4096,2048]{1,0:T(8,128)(2,1)} %get-tuple-element.682, ...), kind=kOutput, calls=%fused_computation.27.clone.1 | convolution fusion | flops 1074266112 | bytes 18350084 | tf_op jit(solution)/shard_map/while/body/eval_jaxpr/dot_general | solution.py:118
  167.7 5.7 all-reduce.3
  185.2 5.6 all-gather.3.cloned.1.call-done
  196.3 8.8 convolution_convert_fusion.6
  207.8 7.2 all_gather.35
  214.9 9.5 %select_dynamic-update-slice_fusion.2 = (bf16[512,2048]{1,0:T(8,128)(2,1)}, bf16[64,2048]{1,0:T(8,128)(2,1)S(1)}) fusion(bf16[512,2048]{1,0:T(8,128)(2,1)} %get-tuple-element.644, s32[]{:T(128)S(6)} %select_n.328, pred[]{:T(512)S(6)} %and.146, bf16[64,4096]{1,0:T(8,128)(2,1)S(1)} %all_gather.35, bf16[4096,2048]{1,0:T(8,128)(2,1)} %get-tuple-element.682, ...), kind=kOutput, calls=%fused_computation.27.clone.1 | convolution fusion | flops 1074266112 | bytes 18350084 | tf_op jit(solution)/shard_map/while/body/eval_jaxpr/dot_general | solution.py:118
  243.9 5.7 all-reduce.3
  266.6 5.3 dynamic-slice_select_fusion.4
  272.1 8.8 convolution_convert_fusion.6
  283.9 7.2 all_gather.35
  291.1 9.5 %select_dynamic-update-slice_fusion.2 = (bf16[512,2048]{1,0:T(8,128)(2,1)}, bf16[64,2048]{1,0:T(8,128)(2,1)S(1)}) fusion(bf16[512,2048]{1,0:T(8,128)(2,1)} %get-tuple-element.644, s32[]{:T(128)S(6)} %select_n.328, pred[]{:T(512)S(6)} %and.146, bf16[64,4096]{1,0:T(8,128)(2,1)S(1)} %all_gather.35, bf16[4096,2048]{1,0:T(8,128)(2,1)} %get-tuple-element.682, ...), kind=kOutput, calls=%fused_computation.27.clone.1 | convolution fusion | flops 1074266112 | bytes 18350084 | tf_op jit(solution)/shard_map/while/body/eval_jaxpr/dot_general | solution.py:118
  319.2 5.8 all-reduce.3
  336.8 5.6 all-gather.3.cloned.1.call-done
  342.4 5.3 dynamic-slice_select_fusion.4
  347.9 8.8 convolution_convert_fusion.6
  359.3 7.2 all_gather.35
  366.5 9.5 %select_dynamic-update-slice_fusion.2 = (bf16[512,2048]{1,0:T(8,128)(2,1)}, bf16[64,2048]{1,0:T(8,128)(2,1)S(1)}) fusion(bf16[512,2048]{1,0:T(8,128)(2,1)} %get-tuple-element.644, s32[]{:T(128)S(6)} %select_n.328, pred[]{:T(512)S(6)} %and.146, bf16[64,4096]{1,0:T(8,128)(2,1)S(1)} %all_gather.35, bf16[4096,2048]{1,0:T(8,128)(2,1)} %get-tuple-element.682, ...), kind=kOutput, calls=%fused_computation.27.clone.1 | convolution fusion | flops 1074266112 | bytes 18350084 | tf_op jit(solution)/shard_map/while/body/eval_jaxpr/dot_general | solution.py:118
  395.5 5.7 all-reduce.3
  413.0 5.6 all-gather.3.cloned.1.call-done
  418.6 5.3 dynamic-slice_select_fusion.4
  424.1 8.8 convolution_convert_fusion.6
  435.9 7.2 all_gather.35
  443.1 9.5 %select_dynamic-update-slice_fusion.2 = (bf16[512,2048]{1,0:T(8,128)(2,1)}, bf16[64,2048]{1,0:T(8,128)(2,1)S(1)}) fusion(bf16[512,2048]{1,0:T(8,128)(2,1)} %get-tuple-element.644, s32[]{:T(128)S(6)} %select_n.328, pred[]{:T(512)S(6)} %and.146, bf16[64,4096]{1,0:T(8,128)(2,1)S(1)} %all_gather.35, bf16[4096,2048]{1,0:T(8,128)(2,1)} %get-tuple-element.682, ...), kind=kOutput, calls=%fused_computation.27.clone.1 | convolution fusion | flops 1074266112 | bytes 18350084 | tf_op jit(solution)/shard_map/while/body/eval_jaxpr/dot_general | solution.py:118
  471.3 5.7 all-reduce.3
  488.8 5.6 all-gather.3.cloned.1.call-done
  494.4 5.3 dynamic-slice_select_fusion.4
  499.9 8.8 convolution_convert_fusion.6
  511.2 7.2 all_gather.35
  518.4 9.5 %select_dynamic-update-slice_fusion.2 = (bf16[512,2048]{1,0:T(8,128)(2,1)}, bf16[64,2048]{1,0:T(8,128)(2,1)S(1)}) fusion(bf16[512,2048]{1,0:T(8,128)(2,1)} %get-tuple-element.644, s32[]{:T(128)S(6)} %select_n.328, pred[]{:T(512)S(6)} %and.146, bf16[64,4096]{1,0:T(8,128)(2,1)S(1)} %all_gather.35, bf16[4096,2048]{1,0:T(8,128)(2,1)} %get-tuple-element.682, ...), kind=kOutput, calls=%fused_computation.27.clone.1 | convolution fusion | flops 1074266112 | bytes 18350084 | tf_op jit(solution)/shard_map/while/body/eval_jaxpr/dot_general | solution.py:118
  547.4 5.8 all-reduce.3
  565.0 5.5 all-gather.3.cloned.1.call-done
  570.5 5.3 dynamic-slice_select_fusion.4
  576.0 8.8 convolution_convert_fusion.6
  587.8 7.2 all_gather.35
  595.0 9.5 %select_dynamic-update-slice_fusion.2 = (bf16[512,2048]{1,0:T(8,128)(2,1)}, bf16[64,2048]{1,0:T(8,128)(2,1)S(1)}) fusion(bf16[512,2048]{1,0:T(8,128)(2,1)} %get-tuple-element.644, s32[]{:T(128)S(6)} %select_n.328, pred[]{:T(512)S(6)} %and.146, bf16[64,4096]{1,0:T(8,128)(2,1)S(1)} %all_gather.35, bf16[4096,2048]{1,0:T(8,128)(2,1)} %get-tuple-element.682, ...), kind=kOutput, calls=%fused_computation.27.clone.1 | convolution fusion | flops 1074266112 | bytes 18350084 | tf_op jit(solution)/shard_map/while/body/eval_jaxpr/dot_general | solution.py:118
  623.1 5.7 all-reduce.3
  640.7 5.7 all-gather.3.cloned.1.call-done
  646.3 5.3 dynamic-slice_select_fusion.4
  651.8 8.8 convolution_convert_fusion.6
  663.6 7.2 all_gather.35
  670.8 9.5 %select_dynamic-update-slice_fusion.2 = (bf16[512,2048]{1,0:T(8,128)(2,1)}, bf16[64,2048]{1,0:T(8,128)(2,1)S(1)}) fusion(bf16[512,2048]{1,0:T(8,128)(2,1)} %get-tuple-element.644, s32[]{:T(128)S(6)} %select_n.328, pred[]{:T(512)S(6)} %and.146, bf16[64,4096]{1,0:T(8,128)(2,1)S(1)} %all_gather.35, bf16[4096,2048]{1,0:T(8,128)(2,1)} %get-tuple-element.682, ...), kind=kOutput, calls=%fused_computation.27.clone.1 | convolution fusion | flops 1074266112 | bytes 18350084 | tf_op jit(solution)/shard_map/while/body/eval_jaxpr/dot_general | solution.py:118
  699.4 5.7 all-reduce.3
  717.0 5.5 all-gather.3.cloned.1.call-done
  722.5 5.3 dynamic-slice_select_fusion.4
  728.0 8.8 convolution_convert_fusion.6
  739.8 7.2 all_gather.35
  746.9 9.5 %select_dynamic-update-slice_fusion.2 = (bf16[512,2048]{1,0:T(8,128)(2,1)}, bf16[64,2048]{1,0:T(8,128)(2,1)S(1)}) fusion(bf16[512,2048]{1,0:T(8,128)(2,1)} %get-tuple-element.644, s32[]{:T(128)S(6)} %select_n.328, pred[]{:T(512)S(6)} %and.146, bf16[64,4096]{1,0:T(8,128)(2,1)S(1)} %all_gather.35, bf16[4096,2048]{1,0:T(8,128)(2,1)} %get-tuple-element.682, ...), kind=kOutput, calls=%fused_computation.27.clone.1 | convolution fusion | flops 1074266112 | bytes 18350084 | tf_op jit(solution)/shard_map/while/body/eval_jaxpr/dot_general | solution.py:118
  775.6 5.7 all-reduce.3
  798.2 5.3 dynamic-slice_select_fusion.4
  803.7 8.8 convolution_convert_fusion.6
  815.5 7.2 all_gather.35
  822.7 9.5 %select_dynamic-update-slice_fusion.2 = (bf16[512,2048]{1,0:T(8,128)(2,1)}, bf16[64,2048]{1,0:T(8,128)(2,1)S(1)}) fusion(bf16[512,2048]{1,0:T(8,128)(2,1)} %get-tuple-element.644, s32[]{:T(128)S(6)} %select_n.328, pred[]{:T(512)S(6)} %and.146, bf16[64,4096]{1,0:T(8,128)(2,1)S(1)} %all_gather.35, bf16[4096,2048]{1,0:T(8,128)(2,1)} %get-tuple-element.682, ...), kind=kOutput, calls=%fused_computation.27.clone.1 | convolution fusion | flops 1074266112 | bytes 18350084 | tf_op jit(solution)/shard_map/while/body/eval_jaxpr/dot_general | solution.py:118
  850.2 86.3 %all-reduce.6.cloned.1.call-done = bf16[512,2048]{1,0:T(8,128)(2,1)} async-done(((bf16[512,2048]{1,0:T(8,128)(2,1)}), bf16[512,2048]{1,0:T(8,128)(2,1)}) %all-reduce.6.cloned.1.call-update) | async-done | bytes 2097168 | tf_op jit(solution)/shard_map/psum | solution.py:28
  (636 shorter events, 388.4 us)
Async XLA Ops:
  8.0 1.8 copy-start.4
  8.0 1.8 copy-start.2
  8.0 1.8 copy-start.3
  9.9 29.2 %all-gather.3.cloned.1.call-start = ((), (), s32[]{:S(2)}) async-start(), calls=%async_computation.3 | async-start | bytes 1310720 | tf_op jit(solution)/shard_map/while/body/eval_jaxpr/all_gather | solution.py:134
  24.6 6.9 all-to-all-start
  39.1 5.5 copy-start
  72.8 16.3 %collective-permute-start = (bf16[64,2048]{1,0:T(8,128)(2,1)S(1)}, bf16[64,2048]{1,0:T(8,128)(2,1)S(1)}, u32[]{:S(2)}, u32[]{:S(2)}) collective-permute-start(bf16[64,2048]{1,0:T(8,128)(2,1)S(1)} %get-tuple-element.605), channel_id=1, source_target_pairs={{0,1},{1,2},{2,3},{4,5},{5,6},{6,7},{8,9},{9,10},{10,11},{12,13},{... | collective-permute-start | bytes 786440 | tf_op jit(solution)/shard_map/while/body/eval_jaxpr/ppermute | solution.py:23
  77.6 7.9 all-to-all-start.1
  89.1 25.9 %all-gather.3.cloned.1.call-start = ((), (), s32[]{:S(2)}) async-start(), calls=%async_computation.3 | async-start | bytes 1310720 | tf_op jit(solution)/shard_map/while/body/eval_jaxpr/all_gather | solution.py:134
  101.2 6.9 all-to-all-start
  115.0 5.5 copy-start
  149.0 15.9 %collective-permute-start = (bf16[64,2048]{1,0:T(8,128)(2,1)S(1)}, bf16[64,2048]{1,0:T(8,128)(2,1)S(1)}, u32[]{:S(2)}, u32[]{:S(2)}) collective-permute-start(bf16[64,2048]{1,0:T(8,128)(2,1)S(1)} %get-tuple-element.605), channel_id=1, source_target_pairs={{0,1},{1,2},{2,3},{4,5},{5,6},{6,7},{8,9},{9,10},{10,11},{12,13},{... | collective-permute-start | bytes 786440 | tf_op jit(solution)/shard_map/while/body/eval_jaxpr/ppermute | solution.py:23
  153.5 7.9 all-to-all-start.1
  165.0 25.9 %all-gather.3.cloned.1.call-start = ((), (), s32[]{:S(2)}) async-start(), calls=%async_computation.3 | async-start | bytes 1310720 | tf_op jit(solution)/shard_map/while/body/eval_jaxpr/all_gather | solution.py:134
  177.0 6.9 all-to-all-start
  190.8 5.5 copy-start
  224.4 16.7 %collective-permute-start = (bf16[64,2048]{1,0:T(8,128)(2,1)S(1)}, bf16[64,2048]{1,0:T(8,128)(2,1)S(1)}, u32[]{:S(2)}, u32[]{:S(2)}) collective-permute-start(bf16[64,2048]{1,0:T(8,128)(2,1)S(1)} %get-tuple-element.605), channel_id=1, source_target_pairs={{0,1},{1,2},{2,3},{4,5},{5,6},{6,7},{8,9},{9,10},{10,11},{12,13},{... | collective-permute-start | bytes 786440 | tf_op jit(solution)/shard_map/while/body/eval_jaxpr/ppermute | solution.py:23
  229.7 7.9 all-to-all-start.1
  241.2 25.4 %all-gather.3.cloned.1.call-start = ((), (), s32[]{:S(2)}) async-start(), calls=%async_computation.3 | async-start | bytes 1310720 | tf_op jit(solution)/shard_map/while/body/eval_jaxpr/all_gather | solution.py:134
  253.3 6.9 all-to-all-start
  266.6 5.5 copy-start
  300.6 15.8 %collective-permute-start = (bf16[64,2048]{1,0:T(8,128)(2,1)S(1)}, bf16[64,2048]{1,0:T(8,128)(2,1)S(1)}, u32[]{:S(2)}, u32[]{:S(2)}) collective-permute-start(bf16[64,2048]{1,0:T(8,128)(2,1)S(1)} %get-tuple-element.605), channel_id=1, source_target_pairs={{0,1},{1,2},{2,3},{4,5},{5,6},{6,7},{8,9},{9,10},{10,11},{12,13},{... | collective-permute-start | bytes 786440 | tf_op jit(solution)/shard_map/while/body/eval_jaxpr/ppermute | solution.py:23
  305.0 7.9 all-to-all-start.1
  316.5 25.9 %all-gather.3.cloned.1.call-start = ((), (), s32[]{:S(2)}) async-start(), calls=%async_computation.3 | async-start | bytes 1310720 | tf_op jit(solution)/shard_map/while/body/eval_jaxpr/all_gather | solution.py:134
  328.6 6.9 all-to-all-start
  342.4 5.5 copy-start
  376.0 16.7 %collective-permute-start = (bf16[64,2048]{1,0:T(8,128)(2,1)S(1)}, bf16[64,2048]{1,0:T(8,128)(2,1)S(1)}, u32[]{:S(2)}, u32[]{:S(2)}) collective-permute-start(bf16[64,2048]{1,0:T(8,128)(2,1)S(1)} %get-tuple-element.605), channel_id=1, source_target_pairs={{0,1},{1,2},{2,3},{4,5},{5,6},{6,7},{8,9},{9,10},{10,11},{12,13},{... | collective-permute-start | bytes 786440 | tf_op jit(solution)/shard_map/while/body/eval_jaxpr/ppermute | solution.py:23
  381.3 7.9 all-to-all-start.1
  392.8 25.8 %all-gather.3.cloned.1.call-start = ((), (), s32[]{:S(2)}) async-start(), calls=%async_computation.3 | async-start | bytes 1310720 | tf_op jit(solution)/shard_map/while/body/eval_jaxpr/all_gather | solution.py:134
  404.8 6.9 all-to-all-start
  418.6 5.5 copy-start
  452.6 15.9 %collective-permute-start = (bf16[64,2048]{1,0:T(8,128)(2,1)S(1)}, bf16[64,2048]{1,0:T(8,128)(2,1)S(1)}, u32[]{:S(2)}, u32[]{:S(2)}) collective-permute-start(bf16[64,2048]{1,0:T(8,128)(2,1)S(1)} %get-tuple-element.605), channel_id=1, source_target_pairs={{0,1},{1,2},{2,3},{4,5},{5,6},{6,7},{8,9},{9,10},{10,11},{12,13},{... | collective-permute-start | bytes 786440 | tf_op jit(solution)/shard_map/while/body/eval_jaxpr/ppermute | solution.py:23
  457.1 7.9 all-to-all-start.1
  468.5 25.8 %all-gather.3.cloned.1.call-start = ((), (), s32[]{:S(2)}) async-start(), calls=%async_computation.3 | async-start | bytes 1310720 | tf_op jit(solution)/shard_map/while/body/eval_jaxpr/all_gather | solution.py:134
  480.6 6.9 all-to-all-start
  494.4 5.5 copy-start
  527.9 16.8 %collective-permute-start = (bf16[64,2048]{1,0:T(8,128)(2,1)S(1)}, bf16[64,2048]{1,0:T(8,128)(2,1)S(1)}, u32[]{:S(2)}, u32[]{:S(2)}) collective-permute-start(bf16[64,2048]{1,0:T(8,128)(2,1)S(1)} %get-tuple-element.605), channel_id=1, source_target_pairs={{0,1},{1,2},{2,3},{4,5},{5,6},{6,7},{8,9},{9,10},{10,11},{12,13},{... | collective-permute-start | bytes 786440 | tf_op jit(solution)/shard_map/while/body/eval_jaxpr/ppermute | solution.py:23
  533.3 7.9 all-to-all-start.1
  544.7 25.8 %all-gather.3.cloned.1.call-start = ((), (), s32[]{:S(2)}) async-start(), calls=%async_computation.3 | async-start | bytes 1310720 | tf_op jit(solution)/shard_map/while/body/eval_jaxpr/all_gather | solution.py:134
  556.9 6.9 all-to-all-start
  570.5 5.5 copy-start
  604.5 15.9 %collective-permute-start = (bf16[64,2048]{1,0:T(8,128)(2,1)S(1)}, bf16[64,2048]{1,0:T(8,128)(2,1)S(1)}, u32[]{:S(2)}, u32[]{:S(2)}) collective-permute-start(bf16[64,2048]{1,0:T(8,128)(2,1)S(1)} %get-tuple-element.605), channel_id=1, source_target_pairs={{0,1},{1,2},{2,3},{4,5},{5,6},{6,7},{8,9},{9,10},{10,11},{12,13},{... | collective-permute-start | bytes 786440 | tf_op jit(solution)/shard_map/while/body/eval_jaxpr/ppermute | solution.py:23
  608.9 7.9 all-to-all-start.1
  620.4 25.9 %all-gather.3.cloned.1.call-start = ((), (), s32[]{:S(2)}) async-start(), calls=%async_computation.3 | async-start | bytes 1310720 | tf_op jit(solution)/shard_map/while/body/eval_jaxpr/all_gather | solution.py:134
  632.5 6.9 all-to-all-start
  646.3 5.5 copy-start
  680.3 16.4 %collective-permute-start = (bf16[64,2048]{1,0:T(8,128)(2,1)S(1)}, bf16[64,2048]{1,0:T(8,128)(2,1)S(1)}, u32[]{:S(2)}, u32[]{:S(2)}) collective-permute-start(bf16[64,2048]{1,0:T(8,128)(2,1)S(1)} %get-tuple-element.605), channel_id=1, source_target_pairs={{0,1},{1,2},{2,3},{4,5},{5,6},{6,7},{8,9},{9,10},{10,11},{12,13},{... | collective-permute-start | bytes 786440 | tf_op jit(solution)/shard_map/while/body/eval_jaxpr/ppermute | solution.py:23
  685.2 7.9 all-to-all-start.1
  696.7 25.8 %all-gather.3.cloned.1.call-start = ((), (), s32[]{:S(2)}) async-start(), calls=%async_computation.3 | async-start | bytes 1310720 | tf_op jit(solution)/shard_map/while/body/eval_jaxpr/all_gather | solution.py:134
  708.8 6.9 all-to-all-start
  722.5 5.5 copy-start
  756.5 16.4 %collective-permute-start = (bf16[64,2048]{1,0:T(8,128)(2,1)S(1)}, bf16[64,2048]{1,0:T(8,128)(2,1)S(1)}, u32[]{:S(2)}, u32[]{:S(2)}) collective-permute-start(bf16[64,2048]{1,0:T(8,128)(2,1)S(1)} %get-tuple-element.605), channel_id=1, source_target_pairs={{0,1},{1,2},{2,3},{4,5},{5,6},{6,7},{8,9},{9,10},{10,11},{12,13},{... | collective-permute-start | bytes 786440 | tf_op jit(solution)/shard_map/while/body/eval_jaxpr/ppermute | solution.py:23
  761.3 7.9 all-to-all-start.1
  772.9 25.4 %all-gather.3.cloned.1.call-start = ((), (), s32[]{:S(2)}) async-start(), calls=%async_computation.3 | async-start | bytes 1310720 | tf_op jit(solution)/shard_map/while/body/eval_jaxpr/all_gather | solution.py:134
  784.9 6.9 all-to-all-start
  798.2 5.5 copy-start
  832.2 16.4 %collective-permute-start = (bf16[64,2048]{1,0:T(8,128)(2,1)S(1)}, bf16[64,2048]{1,0:T(8,128)(2,1)S(1)}, u32[]{:S(2)}, u32[]{:S(2)}) collective-permute-start(bf16[64,2048]{1,0:T(8,128)(2,1)S(1)} %get-tuple-element.605), channel_id=1, source_target_pairs={{0,1},{1,2},{2,3},{4,5},{5,6},{6,7},{8,9},{9,10},{10,11},{12,13},{... | collective-permute-start | bytes 786440 | tf_op jit(solution)/shard_map/while/body/eval_jaxpr/ppermute | solution.py:23
  837.0 7.9 all-to-all-start.1
  848.6 1.6 copy-start.1
  848.6 87.9 %all-reduce.6.cloned.1.call-start = ((), (), s32[]{:S(2)}) async-start(), calls=%async_computation.2 | async-start | bytes 4194304 | tf_op jit(solution)/shard_map/psum | solution.py:28
Sparse Core Ops, SparseCore 0:
  22.0 17.0 all-gather.2
  98.6 16.2 all-gather.2
  174.5 16.2 all-gather.2
  250.8 15.7 all-gather.2
  326.1 16.2 all-gather.2
  402.3 16.2 all-gather.2
  478.1 16.2 all-gather.2
  554.3 16.1 all-gather.2
  630.0 16.3 all-gather.2
  706.3 16.1 all-gather.2
  782.4 15.7 all-gather.2
Sparse Core Ops, SparseCore 1:
  851.5 85.0 all-reduce.5
